TPU v7x, 32 devices: a whole 2x2x4 slice. The times are simulated.
32 devices in a mesh: row: 8 (over z, x), col: 4 (over y, core).
Axes of the slice: x: 2, y: 2, z: 4, core: 2. Of those that a mesh axis runs over, the one named last changes fastest.
Arguments:
- t2_amps: bfloat16 [16384, 49152], P('row', 'col'), may hold values from -0.5 to 0.5
- l2_amps: bfloat16 [256, 49152], P('row', 'col'), may hold values from -0.02734375 to 0.02734375
Outputs:
- ladder: bfloat16 [256, 49152], P('row', 'col')
All inputs are finite; a program needn't handle non-finite values.
Results may differ from a plain program's by a relative error of at most 0.0044.
Values may be sent and summed in bfloat16 or wider, within the bound.
A program may use at most 128 MiB of HBM per device.

v0:
```python
import jax
import jax.numpy as jnp
from jax import lax
from jax.sharding import PartitionSpec as P


def on_device(t2_amps, l2_amps):
    partial_value = jnp.dot(
        t2_amps,
        lax.all_gather(l2_amps, "row", axis=0, tiled=True).T,
        preferred_element_type=jnp.float32,
    )
    oooo = lax.psum(partial_value, "col")
    oooo_half = oooo.astype(jnp.bfloat16)
    ladder = lax.psum_scatter(
        lax.dot_general(
            oooo_half, t2_amps, (((0,), (0,)), ((), ())), preferred_element_type=jnp.float32
        ),
        "row",
        scatter_dimension=0,
        tiled=True,
    )
    return ladder.astype(jnp.bfloat16)


def solution(mesh):
    return jax.shard_map(
        on_device,
        mesh=mesh,
        in_specs=(P("row", "col"), P("row", "col")),
        out_specs=P("row", "col"),
        check_vma=False,
    )
```

profile of v0, /device:TPU:0, one launch (start us, length us, event | category | flops | bytes accessed | tf_op | source)
XLA Modules:
  0.0 413.1 jit_solution(6841744538810563476)
XLA Ops:
  6.5 0.0 all-gather.2.cloned.1.call-start
  6.5 0.7 all-gather.2.cloned.1.call-update
  7.3 0.0 reduce-scatter.2.cloned.1.call-start
  7.3 103.7 %all-gather.2.cloned.1.call-done = bf16[256,12288]{1,0:T(8,128)(2,1)} async-done(((bf16[32,12288]{1,0:T(8,128)(2,1)}), bf16[256,12288]{1,0:T(8,128)(2,1)}) %all-gather.2.cloned.1.call-update) | async-done | bytes 6291472 | tf_op jit(solution)/shard_map/all_gather | solution.py:10
  111.0 21.7 %fusion.2 = f32[2048,256]{1,0:T(8,128)S(1)} fusion(bf16[2048,12288]{1,0:T(8,128)(2,1)} %param.2, bf16[256,12288]{1,0:T(8,128)(2,1)} %all-gather.2.cloned.1.call-done), kind=kOutput, calls=%fused_computation.2 | convolution fusion | flops 12884901888 | bytes 58720256 | tf_op jit(solution)/shard_map/dot_general | solution.py:8
  132.6 40.2 %all-reduce.1 = bf16[2048,256]{1,0:T(8,128)(2,1)S(1)} all-reduce(f32[2048,256]{1,0:T(8,128)S(1)} %fusion.2), channel_id=1, replica_groups=mesh['row'=8,'col'=4] {'col'}, use_global_device_ids=true, to_apply=%region_0.0 | all-reduce | flops 524288 | bytes 3145728 | tf_op jit(solution)/shard_map/psum | solution.py:13
  172.8 24.8 %fusion.3 = f32[256,12288]{1,0:T(8,128)} fusion(bf16[2048,256]{1,0:T(8,128)(2,1)S(1)} %all-reduce.1, bf16[2048,12288]{1,0:T(8,128)(2,1)} %param.2), kind=kOutput, calls=%fused_computation.3 | convolution fusion | flops 12884901888 | bytes 63963136 | tf_op jit(solution)/shard_map/dot_general | solution.py:16
  197.6 0.0 reduce-scatter.2.cloned.1.call-update
  197.6 206.2 %reduce-scatter.2.cloned.1.call-done = f32[32,12288]{1,0:T(8,128)} async-done(((f32[256,12288]{1,0:T(8,128)}), f32[32,12288]{1,0:T(8,128)}) %reduce-scatter.2.cloned.1.call-update) | async-done | bytes 1572880 | tf_op jit(solution)/shard_map/reduce_scatter | solution.py:15
  403.9 2.4 convert_element_type.7
Async XLA Ops:
  6.5 104.4 %all-gather.2.cloned.1.call-start = ((), (), s32[]{:S(2)}) async-start(), calls=%async_computation.1 | async-start | bytes 7077888 | tf_op jit(solution)/shard_map/all_gather | solution.py:10
  7.3 396.6 %reduce-scatter.2.cloned.1.call-start = ((), (), s32[]{:S(2)}) async-start(), calls=%async_computation.2 | async-start | bytes 14155776 | tf_op jit(solution)/shard_map/reduce_scatter | solution.py:15
Sparse Core Ops, SparseCore 0:
  9.5 101.4 all-gather.1
  197.7 206.0 reduce-scatter.1
where the time goes:
time: 413 us
  waiting for transfers between devices  311 us (75%)
  matrix products  46.4 us (11%)
  blocking collectives  40.2 us (10%)
  between operations  13.4 us (3%)
    reduce_scatter x1, waiting for transfers between devices, on_device(): lax.psum_scatter(lax.dot_general(oooo_half, t2_amps, (((0,), (0,)), ((),...  206 us
    all_gather x1, waiting for transfers between devices, on_device(): lax.all_gather(l2_amps, 'row', axis=0, tiled=True)  104 us
    psum x1, blocking collectives, on_device(): oooo = lax.psum(partial_value, 'col')  40.2 us
    dot_general x1, matrix products, on_device(): lax.dot_general(oooo_half, t2_amps, (((0,), (0,)), ((), ())), preferred_e...  24.8 us
    dot_general x1, matrix products, on_device(): jnp.dot(t2_amps, lax.all_gather(l2_amps, 'row', axis=0, tiled=True).T, pr...  21.7 us
  transfers between devices with their start and end apart: 2, of which 2 were waited for; matrix products, arithmetic and copies ran while one was open for 0% of the time, Pallas kernels for 0%

commit v1 on v0

--- a/solution.py
+++ b/solution.py
@@ -10,7 +10,10 @@
         lax.all_gather(l2_amps, "row", axis=0, tiled=True).T,
         preferred_element_type=jnp.float32,
     )
-    oooo = lax.psum(partial_value, "col")
+    devices, oooo = (lax.axis_size("col"), partial_value)
+    for far in [1 << k for k in range(devices.bit_length() - 1)]:
+        swap = [(i, i ^ far) for i in range(devices)]
+        oooo = oooo + lax.ppermute(oooo, "col", swap)
     oooo_half = oooo.astype(jnp.bfloat16)
     ladder = lax.psum_scatter(
         lax.dot_general(

time: 413 us -> 426 us (1.031)
  waiting for transfers between devices: 311 us -> 360 us
  blocking collectives: 40.2 us -> 0 us
    ppermute x0 -> x2, waiting for transfers between devices: none -> 50.3 us  [on_device(): oooo = oooo + lax.ppermute(oooo, 'col', swap)]
    psum x1 -> x0, blocking collectives: 40.2 us -> none  [on_device(): oooo = lax.psum(partial_value, 'col')]
  transfers between devices with their start and end apart: 2 -> 4, of which waited for: 2 -> 4; matrix products, arithmetic and copies ran while one was open for 0% -> 0% of each run, Pallas kernels for 0% -> 0%
where the time goes in v1:
time: 426 us
  waiting for transfers between devices  360 us (85%)
  matrix products  47.8 us (11%)
  between operations  13.4 us (3%)
    reduce_scatter x1, waiting for transfers between devices, on_device(): lax.psum_scatter(lax.dot_general(oooo_half, t2_amps, (((0,), (0,)), ((),...  206 us
    all_gather x1, waiting for transfers between devices, on_device(): lax.all_gather(l2_amps, 'row', axis=0, tiled=True)  104 us
    ppermute x2, waiting for transfers between devices, on_device(): oooo = oooo + lax.ppermute(oooo, 'col', swap)  50.3 us
    dot_general x1, matrix products, on_device(): lax.dot_general(oooo_half, t2_amps, (((0,), (0,)), ((), ())), preferred_e...  26.1 us
    dot_general x1, matrix products, on_device(): jnp.dot(t2_amps, lax.all_gather(l2_amps, 'row', axis=0, tiled=True).T, pr...  21.7 us
  transfers between devices with their start and end apart: 4, of which 4 were waited for; matrix products, arithmetic and copies ran while one was open for 0% of the time, Pallas kernels for 0%

profile of v1, /device:TPU:0, one launch (start us, length us, event | category | flops | bytes accessed | tf_op | source)
XLA Modules:
  0.0 426.0 jit_solution(7570361144645282699)
XLA Ops:
  6.5 0.0 all-gather.2.cloned.1.call-start
  6.5 0.7 all-gather.2.cloned.1.call-update
  7.3 0.0 reduce-scatter.2.cloned.1.call-start
  7.3 103.7 %all-gather.2.cloned.1.call-done = bf16[256,12288]{1,0:T(8,128)(2,1)} async-done(((bf16[32,12288]{1,0:T(8,128)(2,1)}), bf16[256,12288]{1,0:T(8,128)(2,1)}) %all-gather.2.cloned.1.call-update) | async-done | bytes 6291472 | tf_op jit(solution)/shard_map/all_gather | solution.py:10
  111.0 21.7 %fusion.1 = f32[2048,256]{1,0:T(8,128)S(1)} fusion(bf16[2048,12288]{1,0:T(8,128)(2,1)} %param.2, bf16[256,12288]{1,0:T(8,128)(2,1)} %all-gather.2.cloned.1.call-done), kind=kOutput, calls=%fused_computation.2 | convolution fusion | flops 12884901888 | bytes 58720256 | tf_op jit(solution)/shard_map/dot_general | solution.py:8
  132.6 0.1 collective-permute-start
  132.7 4.1 collective-permute-done
  136.9 0.3 add.8
  137.1 1.5 collective-permute-start.1
  138.7 46.2 %collective-permute-done.1 = f32[2048,256]{1,0:T(8,128)S(1)} collective-permute-done((f32[2048,256]{1,0:T(8,128)S(1)}, f32[2048,256]{1,0:T(8,128)S(1)}, u32[]{:S(2)}, u32[]{:S(2)}) %collective-permute-start.1) | collective-permute-done | bytes 2097184 | tf_op jit(solution)/shard_map/ppermute | solution.py:16
  184.9 26.1 %fusion = f32[256,12288]{1,0:T(8,128)} fusion(bf16[2048,12288]{1,0:T(8,128)(2,1)} %param.2, f32[2048,256]{1,0:T(8,128)S(1)} %add.8, f32[2048,256]{1,0:T(8,128)S(1)} %collective-permute-done.1), kind=kOutput, calls=%fused_computation.1 | convolution fusion | flops 12885950464 | bytes 67108864 | tf_op jit(solution)/shard_map/dot_general | solution.py:19
  211.0 0.0 reduce-scatter.2.cloned.1.call-update
  211.0 205.8 %reduce-scatter.2.cloned.1.call-done = f32[32,12288]{1,0:T(8,128)} async-done(((f32[256,12288]{1,0:T(8,128)}), f32[32,12288]{1,0:T(8,128)}) %reduce-scatter.2.cloned.1.call-update) | async-done | bytes 1572880 | tf_op jit(solution)/shard_map/reduce_scatter | solution.py:18
  416.8 2.4 convert_element_type.7
Async XLA Ops:
  6.5 104.4 %all-gather.2.cloned.1.call-start = ((), (), s32[]{:S(2)}) async-start(), calls=%async_computation.1 | async-start | bytes 7077888 | tf_op jit(solution)/shard_map/all_gather | solution.py:10
  7.3 409.5 %reduce-scatter.2.cloned.1.call-start = ((), (), s32[]{:S(2)}) async-start(), calls=%async_computation.2 | async-start | bytes 14155776 | tf_op jit(solution)/shard_map/reduce_scatter | solution.py:18
  132.6 4.2 collective-permute-start
  137.1 47.7 %collective-permute-start.1 = (f32[2048,256]{1,0:T(8,128)S(1)}, f32[2048,256]{1,0:T(8,128)S(1)}, u32[]{:S(2)}, u32[]{:S(2)}) collective-permute-start(f32[2048,256]{1,0:T(8,128)S(1)} %add.8), channel_id=1, source_target_pairs={{0,2},{1,3},{2,0},{3,1},{4,6},{5,7},{6,4},{7,5},{8,10},{9,11},{10,... | collective-permute-start | bytes 6291464 | tf_op jit(solution)/shard_map/ppermute | solution.py:16
Sparse Core Ops, SparseCore 0:
  9.5 101.4 all-gather.1
  211.1 205.6 reduce-scatter.1
